TPU v7x, 32 devices: a 4x4x1 block of a 4x4x8 slice. The times are simulated.
32 devices in a mesh: dp: 1 (over z), row: 4 (over y), col: 8 (over x, core).
Axes of the slice: x: 4, y: 4, z: 1, core: 2. Of those that a mesh axis runs over, the one named last changes fastest.
The devices are a block of a 4x4x8 slice.
Arguments:
- x_in: bfloat16 [16, 512, 2560], P('dp', None, ('row', 'col'))
- ln_gain: bfloat16 [2, 2560], P(None, ('row', 'col'))
- w_in: bfloat16 [2, 2560, 23040], P(None, 'row', 'col')
- w_kv: bfloat16 [2, 2560, 160], P(None, 'row', 'col')
- w_out: bfloat16 [2, 12800, 2560], P(None, 'col', 'row')
Outputs:
- output 1: bfloat16 [16, 512, 2560], P('dp', None, ('row', 'col'))
- output 2: bfloat16 [2, 2, 16, 512, 80], P(None, None, 'dp', ('row', 'col'))
All inputs are finite; a program needn't handle non-finite values.
Results may differ from a plain program's by a relative error of at most 0.0163933.
Values are sent between devices in bfloat16 or wider.
A program may use at most 768 MiB of HBM per device.

v0:
```python
import jax
import jax.numpy as jnp
from jax import lax
from jax.sharding import PartitionSpec as P

LN_EPS = 1e-6


def rope_tables(positions, head_dim):
    half_dim = head_dim // 2
    inv_freq = 1.0 / (10000.0 ** (jnp.arange(half_dim, dtype=jnp.float32) * 2.0 / head_dim))
    angles = positions.astype(jnp.float32)[:, None] * inv_freq[None, :]
    return jnp.cos(angles), jnp.sin(angles)


def apply_rope(values, cos_tab, sin_tab):
    half_dim = values.shape[-1] // 2
    lower_half = values[..., :half_dim]
    upper_half = values[..., half_dim:]
    return jnp.concatenate([lower_half * cos_tab - upper_half * sin_tab, upper_half * cos_tab + lower_half * sin_tab], axis=-1)


def solution(mesh):
    row_size = mesh.shape["row"]
    col_size = mesh.shape["col"]
    act_spec = P("dp", None, ("row", "col"))
    weight_spec = P(None, "row", "col")

    def device_fn(x_loc, gain_loc, w_in_loc, w_kv_loc, w_out_loc):
        n_layers = w_in_loc.shape[0]
        n_batch, seq_len, d_local = x_loc.shape
        d_model = d_local * row_size * col_size
        e_block = w_in_loc.shape[2]
        r_block = w_out_loc.shape[1]
        f_block = e_block - r_block
        q_block = r_block - f_block
        head_dim = w_kv_loc.shape[2] * col_size // 2
        heads_local = q_block // head_dim
        seq_local = seq_len // (row_size * col_size)
        shard_index = lax.axis_index("row") * col_size + lax.axis_index("col")
        positions = jnp.arange(seq_len)
        cos_tab, sin_tab = rope_tables(positions, head_dim)
        causal = positions[None, :] <= positions[:, None]
        hidden = x_loc
        kv_outs = []
        for layer_idx in range(n_layers):
            hidden_f32 = hidden.astype(jnp.float32)
            tok_sum = lax.psum(jnp.sum(hidden_f32, axis=-1, keepdims=True), ("row", "col"))
            centered = hidden_f32 - tok_sum / d_model
            sq_sum = lax.psum(jnp.sum(centered * centered, axis=-1, keepdims=True), ("row", "col"))
            normed = (centered * lax.rsqrt(sq_sum / d_model + LN_EPS) * gain_loc[layer_idx].astype(jnp.float32)).astype(jnp.bfloat16)
            normed_row = lax.all_gather(normed, "col", axis=2, tiled=True)
            part_main = jnp.einsum("bsd,de->bse", normed_row, w_in_loc[layer_idx], preferred_element_type=jnp.float32).astype(jnp.bfloat16)
            part_kv = jnp.einsum("bsd,de->bse", normed_row, w_kv_loc[layer_idx], preferred_element_type=jnp.float32).astype(jnp.bfloat16)
            main_proj, kv_piece = lax.psum((part_main, part_kv), "row")
            kv_proj = lax.all_gather(kv_piece, "col", axis=2, tiled=True)
            query = main_proj[..., :q_block].reshape(n_batch, seq_len, heads_local, head_dim)
            gate_val = main_proj[..., q_block:q_block + f_block]
            up_val = main_proj[..., q_block + f_block:]
            q_rot = (apply_rope(query.astype(jnp.float32), cos_tab[:, None, :], sin_tab[:, None, :]) * head_dim ** -0.5).astype(jnp.bfloat16)
            k_rot = apply_rope(kv_proj[..., :head_dim].astype(jnp.float32), cos_tab, sin_tab).astype(jnp.bfloat16)
            v_val = kv_proj[..., head_dim:]
            scores = jnp.einsum("crie,cle->cirl", q_rot, k_rot, preferred_element_type=jnp.float32)
            scores = jnp.where(causal, scores, -1e30)
            attn_prob = jax.nn.softmax(scores, axis=-1).astype(jnp.bfloat16)
            attn_out = jnp.einsum("cirl,cle->crie", attn_prob, v_val, preferred_element_type=jnp.float32).astype(jnp.bfloat16).reshape(n_batch, seq_len, q_block)
            mlp_out = (jax.nn.silu(gate_val.astype(jnp.float32)) * up_val.astype(jnp.float32)).astype(jnp.bfloat16)
            joined = jnp.concatenate([attn_out, mlp_out], axis=2)
            part_out = jnp.einsum("bsr,rd->bsd", joined, w_out_loc[layer_idx], preferred_element_type=jnp.float32).astype(jnp.bfloat16)
            update = lax.psum_scatter(part_out, "col", scatter_dimension=2, tiled=True)
            hidden = hidden + update
            kv_outs.append(lax.dynamic_slice_in_dim(jnp.stack([k_rot, v_val]), shard_index * seq_local, seq_local, axis=2))
        return hidden, jnp.stack(kv_outs)

    return jax.shard_map(device_fn, mesh=mesh, in_specs=(act_spec, P(None, ("row", "col")), weight_spec, weight_spec, P(None, "col", "row")), out_specs=(act_spec, P(None, None, "dp", ("row", "col"), None)), check_vma=False)
```

profile of v0, /device:TPU:97, one launch (start us, length us, event | category | flops | bytes accessed | tf_op | source)
XLA Modules:
  0.0 2357.4 jit_solution(1020968021623619907)
XLA Ops:
  10.1 49.9 %psum.56 = f32[16,512,1]{1,0,2:T(8,128)S(1)} all-reduce(f32[16,512,1]{1,0,2:T(8,128)S(1)} %bitcast.180), channel_id=1, replica_groups=mesh['dp'=1,'row'=4,'col'=8] {'row','col'}, use_global_device_ids=true, to_apply=%region_1.0 | all-reduce | flops 8192 | bytes 65536 | tf_op jit(solution)/shard_map/psum | solution.py:48
  61.8 43.6 %psum.57 = f32[16,512,1]{1,0,2:T(8,128)S(1)} all-reduce(f32[16,512,1]{1,0,2:T(8,128)S(1)} %bitcast.178), channel_id=1, replica_groups=mesh['dp'=1,'row'=4,'col'=8] {'row','col'}, use_global_device_ids=true, to_apply=%region_3.0 | all-reduce | flops 8192 | bytes 65536 | tf_op jit(solution)/shard_map/psum | solution.py:50
  105.3 2.8 fusion.55
  109.5 53.4 %all-gather.5.cloned.1.call-done = bf16[16,512,640]{1,2,0:T(8,128)(2,1)} async-done(((bf16[16,512,80]{1,2,0:T(8,128)(2,1)}), bf16[16,512,640]{1,2,0:T(8,128)(2,1)}) %all-gather.5.cloned.1.call-update) | async-done | bytes 10485776 | tf_op jit(solution)/shard_map/all_gather | solution.py:52
  162.9 6.2 convolution_convert_fusion.3
  169.1 44.9 %convolution_convert_fusion.1 = bf16[16,512,2880]{1,2,0:T(8,128)(2,1)} fusion(bf16[16,512,640]{1,2,0:T(8,128)(2,1)} %all-gather.5.cloned.1.call-done, bf16[2,640,2880]{1,2,0:T(8,128)(2,1)} %param.7), kind=kOutput, calls=%fused_computation.31 | convolution fusion | flops 30222581760 | bytes 61358080 | tf_op jit(solution)/shard_map/bsd,de->bse/dot_general | solution.py:53
  214.6 785.2 %all-reduce.7.cloned.1.call-done = (bf16[16,512,2880]{1,2,0:T(8,128)(2,1)}, bf16[16,512,20]{1,2,0:T(8,128)(2,1)}) async-done(((bf16[16,512,2880]{1,2,0:T(8,128)(2,1)}, bf16[16,512,20]{1,2,0:T(8,128)(2,1)}), (bf16[16,512,2880]{1,2,0:T(8,128)(2,1)}, bf16[16,512,20]{1,2,0:T(8,128)(2,1)})) %all-reduce.7.cloned.1.call-update) | async-done | bytes 47513616 | tf_op jit(solution)/shard_map/psum | solution.py:55
  1002.0 26.3 %fusion.13 = bf16[16,512,1280]{1,2,0:T(8,128)(2,1)} fusion(bf16[16,512,2880]{1,2,0:T(8,128)(2,1)} %get-tuple-element.4), kind=kLoop, calls=%fused_computation.23 | loop fusion | flops 83886080 | bytes 62914560 | tf_op jit(solution)/shard_map/convert_element_type | solution.py:67
  1028.3 3.0 slice.108
  1032.8 6.0 multiply_subtract_fusion.1
  1038.8 1.9 fusion.121
  1042.0 22.2 fusion.123
  1064.3 31.3 %fusion.49 = bf16[16,80,4,512]{3,1,2,0:T(8,128)(2,1)} fusion(f32[16,4,512]{2,1,0:T(4,128)S(1)} %fusion.123, pred[512,512]{0,1:T(8,128)(4,1)S(1)} %iota_compare_fusion, bf16[16,512,80]{1,0,2:T(8,128)(2,1)S(1)} %get-tuple-element.18, bf16[16,512,40]{1,2,0:T(8,128)(2,1)S(1)} %get-tuple-element.15, bf16[16,512,40]{1,2,0:T(8,128)(2,1)S(1)} %get-tuple-element.14, ...), kind=kOutput, calls=%fused_computation.65 | convolution fusion | flops 5448958464 | bytes 18743296 | tf_op jit(solution)/shard_map/cirl,cle->crie/dot_general | solution.py:66
  1095.5 25.0 %fusion.37 = bf16[16,512,640]{1,2,0:T(8,128)(2,1)} fusion(bf16[16,512,1280]{1,2,0:T(8,128)(2,1)} %fusion.13, bf16[16,512,320]{1,2,0:T(8,128)(2,1)} %bitcast.182, bf16[2,1600,640]{2,1,0:T(8,128)(2,1)} %param.9), kind=kOutput, calls=%fused_computation.47 | convolution fusion | flops 16834887680 | bytes 38748160 | tf_op jit(solution)/shard_map/bsr,rd->bsd/dot_general | solution.py:69
  1120.9 60.0 %reduce-scatter.3.cloned.1.call-done = bf16[16,512,80]{1,2,0:T(8,128)(2,1)} async-done(((bf16[16,512,640]{1,2,0:T(8,128)(2,1)}), bf16[16,512,80]{1,2,0:T(8,128)(2,1)}) %reduce-scatter.3.cloned.1.call-update) | async-done | bytes 1310736 | tf_op jit(solution)/shard_map/reduce_scatter | solution.py:70
  1182.8 45.7 %psum.60 = f32[16,512,1]{1,0,2:T(8,128)S(1)} all-reduce(f32[16,512,1]{1,0,2:T(8,128)S(1)} %bitcast.177), channel_id=1, replica_groups=mesh['dp'=1,'row'=4,'col'=8] {'row','col'}, use_global_device_ids=true, to_apply=%region_10.11 | all-reduce | flops 8192 | bytes 65536 | tf_op jit(solution)/shard_map/psum | solution.py:48
  1228.9 44.0 %psum.61 = f32[16,512,1]{1,0,2:T(8,128)S(1)} all-reduce(f32[16,512,1]{1,0,2:T(8,128)S(1)} %bitcast.179), channel_id=1, replica_groups=mesh['dp'=1,'row'=4,'col'=8] {'row','col'}, use_global_device_ids=true, to_apply=%region_12.13 | all-reduce | flops 8192 | bytes 65536 | tf_op jit(solution)/shard_map/psum | solution.py:50
  1274.6 54.7 %all-gather.9.cloned.1.call-done = bf16[16,512,640]{1,2,0:T(8,128)(2,1)} async-done(((bf16[16,512,80]{1,2,0:T(8,128)(2,1)}), bf16[16,512,640]{1,2,0:T(8,128)(2,1)}) %all-gather.9.cloned.1.call-update) | async-done | bytes 10485776 | tf_op jit(solution)/shard_map/all_gather | solution.py:52
  1329.3 44.9 %convolution_convert_fusion = bf16[16,512,2880]{1,2,0:T(8,128)(2,1)} fusion(bf16[16,512,640]{1,2,0:T(8,128)(2,1)} %all-gather.9.cloned.1.call-done, bf16[2,640,2880]{1,2,0:T(8,128)(2,1)} %param.7), kind=kOutput, calls=%fused_computation.30 | convolution fusion | flops 30222581760 | bytes 61358080 | tf_op jit(solution)/shard_map/bsd,de->bse/dot_general | solution.py:53
  1374.2 6.2 convolution_convert_fusion.2
  1380.6 785.7 %all-reduce.5.cloned.1.call-done = (bf16[16,512,2880]{1,2,0:T(8,128)(2,1)}, bf16[16,512,20]{1,2,0:T(8,128)(2,1)}) async-done(((bf16[16,512,2880]{1,2,0:T(8,128)(2,1)}, bf16[16,512,20]{1,2,0:T(8,128)(2,1)}), (bf16[16,512,2880]{1,2,0:T(8,128)(2,1)}, bf16[16,512,20]{1,2,0:T(8,128)(2,1)})) %all-reduce.5.cloned.1.call-update) | async-done | bytes 47513616 | tf_op jit(solution)/shard_map/psum | solution.py:55
  2166.3 1.8 copy.23
  2168.7 26.3 %fusion.12 = bf16[16,512,1280]{1,2,0:T(8,128)(2,1)} fusion(bf16[16,512,2880]{1,2,0:T(8,128)(2,1)} %get-tuple-element.2), kind=kLoop, calls=%fused_computation.22 | loop fusion | flops 83886080 | bytes 62914560 | tf_op jit(solution)/shard_map/convert_element_type | solution.py:67
  2195.0 3.0 slice.117
  2199.5 6.0 multiply_subtract_fusion
  2205.5 1.9 fusion.120
  2208.7 22.2 fusion.128
  2231.0 31.0 %fusion.48 = bf16[16,80,4,512]{3,1,2,0:T(8,128)(2,1)} fusion(f32[16,4,512]{2,1,0:T(4,128)S(1)} %fusion.128, pred[512,512]{0,1:T(8,128)(4,1)S(1)} %iota_compare_fusion, bf16[16,512,80]{1,0,2:T(8,128)(2,1)S(1)} %get-tuple-element.16, bf16[16,512,40]{1,2,0:T(8,128)(2,1)S(1)} %get-tuple-element.13, bf16[16,512,40]{1,2,0:T(8,128)(2,1)S(1)} %get-tuple-element.12, ...), kind=kOutput, calls=%fused_computation.64 | convolution fusion | flops 5448958464 | bytes 18743296 | tf_op jit(solution)/shard_map/cirl,cle->crie/dot_general | solution.py:66
  2262.0 25.2 %fusion.34 = bf16[16,512,640]{1,2,0:T(8,128)(2,1)} fusion(bf16[16,512,1280]{1,2,0:T(8,128)(2,1)} %fusion.12, bf16[16,512,320]{1,2,0:T(8,128)(2,1)} %bitcast.181, bf16[2,1600,640]{2,1,0:T(8,128)(2,1)} %param.9), kind=kOutput, calls=%fused_computation.46 | convolution fusion | flops 16834887680 | bytes 38748160 | tf_op jit(solution)/shard_map/bsr,rd->bsd/dot_general | solution.py:69
  2289.3 2.1 fusion.75
  2295.7 51.9 %reduce-scatter.5.cloned.1.call-done = bf16[16,512,80]{1,2,0:T(8,128)(2,1)} async-done(((bf16[16,512,640]{1,2,0:T(8,128)(2,1)}), bf16[16,512,80]{1,2,0:T(8,128)(2,1)}) %reduce-scatter.5.cloned.1.call-update) | async-done | bytes 1310736 | tf_op jit(solution)/shard_map/reduce_scatter | solution.py:70
  2347.6 2.8 add.67
  (80 shorter events, 25.2 us)
Async XLA Ops:
  7.2 101.6 %copy-start.14 = (bf16[2,640,20]{1,0,2:T(2,128)(2,1)S(1)}, bf16[2,640,20]{1,0,2:T(2,128)(2,1)}, u32[]{:S(2)}) copy-start(bf16[2,640,20]{1,0,2:T(2,128)(2,1)} %param.8) | copy-start | bytes 153604
  7.2 155.7 %all-gather.5.cloned.1.call-start = ((), (), s32[]{:S(2)}) async-start(), calls=%async_computation.2 | async-start | bytes 11796480 | tf_op jit(solution)/shard_map/all_gather | solution.py:52
  108.2 891.6 %all-reduce.7.cloned.1.call-start = ((), (), s32[]{:S(2)}) async-start(), calls=%async_computation.9 | async-start | bytes 95158272 | tf_op jit(solution)/shard_map/psum | solution.py:55
  214.1 824.8 %all-gather.7.cloned.1.call-start = ((), (), s32[]{:S(2)}) async-start(), calls=%async_computation.3 | async-start | bytes 2949120 | tf_op jit(solution)/shard_map/all_gather | solution.py:56
  214.6 826.9 %copy-start.10 = (f32[512,40]{0,1:T(8,128)}, f32[512,40]{0,1:T(8,128)S(1)}, u32[]{:S(2)}) copy-start(f32[512,40]{0,1:T(8,128)S(1)} %get-tuple-element.22) | copy-start | bytes 245764
  214.6 826.9 %copy-start.12 = (f32[512,40]{0,1:T(8,128)}, f32[512,40]{0,1:T(8,128)S(1)}, u32[]{:S(2)}) copy-start(f32[512,40]{0,1:T(8,128)S(1)} %get-tuple-element.23) | copy-start | bytes 245764
  1001.7 179.2 %reduce-scatter.3.cloned.1.call-start = ((), (), s32[]{:S(2)}) async-start(), calls=%async_computation.4 | async-start | bytes 11796480 | tf_op jit(solution)/shard_map/reduce_scatter | solution.py:70
  1040.8 23.5 copy-start.3
  1042.0 22.3 copy-start.5
  1042.0 22.3 copy-start.7
  1120.6 60.4 %copy-start = (bf16[16,512,80]{1,2,0:T(8,128)(2,1)S(1)}, bf16[16,512,80]{1,2,0:T(8,128)(2,1)}, u32[]{:S(2)}) copy-start(bf16[16,512,80]{1,2,0:T(8,128)(2,1)} %param.5) | copy-start | bytes 3932164
  1120.7 152.3 %copy-start.16 = (f32[80]{0:T(128)S(1)}, f32[80]{0:T(128)}, u32[]{:S(2)}) copy-start(f32[80]{0:T(128)} %get-tuple-element.24) | copy-start | bytes 964
  1120.7 208.6 %all-gather.9.cloned.1.call-start = ((), (), s32[]{:S(2)}) async-start(), calls=%async_computation.5 | async-start | bytes 11796480 | tf_op jit(solution)/shard_map/all_gather | solution.py:52
  1182.8 191.4 %copy-start.1 = (bf16[16,512,80]{1,2,0:T(8,128)(2,1)}, bf16[16,512,80]{1,2,0:T(8,128)(2,1)S(1)}, u32[]{:S(2)}) copy-start(bf16[16,512,80]{1,2,0:T(8,128)(2,1)S(1)} %get-tuple-element.7) | copy-start | bytes 3932164
  1274.5 99.7 %copy-start.15 = (bf16[1,640,20]{1,0,2:T(2,128)(2,1)S(1)}, bf16[1,640,20]{1,0,2:T(2,128)(2,1)}, u32[]{:S(2)}) copy-start(bf16[1,640,20]{1,0,2:T(2,128)(2,1)} %get-tuple-element.20) | copy-start | bytes 76804
  1274.5 891.8 %all-reduce.5.cloned.1.call-start = ((), (), s32[]{:S(2)}) async-start(), calls=%async_computation.8 | async-start | bytes 95158272 | tf_op jit(solution)/shard_map/psum | solution.py:55
  1380.5 825.0 %all-gather.11.cloned.1.call-start = ((), (), s32[]{:S(2)}) async-start(), calls=%async_computation.6 | async-start | bytes 2949120 | tf_op jit(solution)/shard_map/all_gather | solution.py:56
  2168.2 179.4 %reduce-scatter.5.cloned.1.call-start = ((), (), s32[]{:S(2)}) async-start(), calls=%async_computation.7 | async-start | bytes 11796480 | tf_op jit(solution)/shard_map/reduce_scatter | solution.py:70
  2198.0 1.5 copy-start.11
  2198.0 1.5 copy-start.13
  2208.7 22.2 copy-start.8
  2208.7 22.2 copy-start.9
  2287.2 1.3 copy-start.4
  2287.2 2.0 copy-start.6
  2289.3 58.3 %copy-start.2 = (bf16[16,512,80]{1,2,0:T(8,128)(2,1)S(1)}, bf16[16,512,80]{1,2,0:T(8,128)(2,1)}, u32[]{:S(2)}) copy-start(bf16[16,512,80]{1,2,0:T(8,128)(2,1)} %copy-done.1) | copy-start | bytes 3932164
Sparse Core Ops, SparseCore 0:
  108.3 54.4 all-gather.4
  214.2 785.6 all-reduce.6
  1002.0 24.5 all-gather.6
  1120.8 60.1 reduce-scatter.2
  1274.6 54.6 all-gather.8
  1380.6 785.6 all-reduce.4
  2168.3 24.5 all-gather.10
  2287.4 60.1 reduce-scatter.4
where the time goes:
time: 2360 us
  waiting for transfers between devices  1790 us (76%)
  matrix products  259 us (11%)
  blocking collectives  183 us (8%)
  other arithmetic  88.5 us (4%)
    psum x2, waiting for transfers between devices, device_fn(): main_proj, kv_piece = lax.psum((part_main, part_kv), 'row')  1570 us
    reduce_scatter x2, waiting for transfers between devices, device_fn(): update = lax.psum_scatter(part_out, 'col', scatter_dimension=2, tiled=True)  112 us
    all_gather x2, waiting for transfers between devices, device_fn(): normed_row = lax.all_gather(normed, 'col', axis=2, tiled=True)  108 us
    psum x2, blocking collectives, device_fn(): lax.psum(jnp.sum(hidden_f32, axis=-1, keepdims=True), ('row', 'col'))  95.7 us
    dot_general x2, matrix products, device_fn(): jnp.einsum('bsd,de->bse', normed_row, w_in_loc[layer_idx], preferred_elem...  89.8 us
    psum x2, blocking collectives, device_fn(): lax.psum(jnp.sum(centered * centered, axis=-1, keepdims=True), ('row', 'c...  87.5 us
    dot_general x2, matrix products, device_fn(): jnp.einsum('cirl,cle->crie', attn_prob, v_val, preferred_element_type=jnp...  62.3 us
    convert_element_type x2, other arithmetic, device_fn(): (jax.nn.silu(gate_val.astype(jnp.float32)) * up_val.astype(jnp.float32))....  52.6 us
  transfers between devices with their start and end apart: 8, of which 6 were waited for; matrix products, arithmetic and copies ran while one was open for 3% of the time, Pallas kernels for 0%

commit v1 on v0

v1 whole, which is shorter than its diff:
```python
import functools

import jax
import jax.numpy as jnp
from jax import lax
from jax.experimental import pallas as pl
from jax.experimental.pallas import tpu as pltpu
from jax.sharding import PartitionSpec as P

LN_EPS = 1e-6
MESH = pl.DeviceIdType.MESH
ANY = pl.BlockSpec(memory_space=pl.ANY)


def rope_tables(positions, head_dim):
    half_dim = head_dim // 2
    inv_freq = 1.0 / (10000.0 ** (jnp.arange(half_dim, dtype=jnp.float32) * 2.0 / head_dim))
    angles = positions.astype(jnp.float32)[:, None] * inv_freq[None, :]
    return jnp.cos(angles), jnp.sin(angles)


def apply_rope(values, cos_tab, sin_tab):
    half_dim = values.shape[-1] // 2
    lower_half = values[..., :half_dim]
    upper_half = values[..., half_dim:]
    return jnp.concatenate([lower_half * cos_tab - upper_half * sin_tab, upper_half * cos_tab + lower_half * sin_tab], axis=-1)


def remote(src, dst, send_sem, recv_sem, **where):
    return pltpu.make_async_remote_copy(src_ref=src, dst_ref=dst, send_sem=send_sem, recv_sem=recv_sem, device_id=where, device_id_type=MESH)


def comm_params(collective_id, vmem=None):
    return pltpu.CompilerParams(collective_id=collective_id, has_side_effects=True, vmem_limit_bytes=vmem)


def exchange_kernel(n_row, n_col, with_rows, *refs):
    if with_rows:
        send, extra, out, extra_out, local_sem, ssem, rsem, local_sem2, ssem2, rsem2 = refs
    else:
        send, out, local_sem, ssem, rsem = refs
    row, col = lax.axis_index("row"), lax.axis_index("col")
    n = n_row * n_col
    me = row * n_col + col
    barrier = pltpu.get_barrier_semaphore()

    def greet(k, carry):
        dest = lax.rem(me + k, n)
        pl.semaphore_signal(barrier, inc=1, device_id={"row": dest // n_col, "col": lax.rem(dest, n_col)}, device_id_type=MESH)
        return carry

    lax.fori_loop(1, n, greet, 0)
    pl.semaphore_wait(barrier, n - 1)

    def copy_to(k):
        dest = lax.rem(me + k, n)
        return remote(send.at[dest], out.at[me], ssem.at[k], rsem.at[k], row=dest // n_col, col=lax.rem(dest, n_col))

    def copy_from(k):
        source = lax.rem(me + n - k, n)
        return remote(send.at[source], out.at[source], ssem.at[k], rsem.at[k], row=row, col=col)

    def rows_to(j):
        dest = lax.rem(row + j, n_row)
        return remote(extra.at[dest], extra_out.at[row], ssem2.at[j], rsem2.at[j], row=dest, col=col)

    def rows_from(j):
        source = lax.rem(row + n_row - j, n_row)
        return remote(extra.at[source], extra_out.at[source], ssem2.at[j], rsem2.at[j], row=row, col=col)

    local = pltpu.make_async_copy(send.at[me], out.at[me], local_sem)
    local.start()

    def start(k, carry):
        copy_to(k).start()
        return carry

    lax.fori_loop(1, n, start, 0)
    if with_rows:
        local2 = pltpu.make_async_copy(extra.at[row], extra_out.at[row], local_sem2)
        local2.start()
        for j in range(1, n_row):
            rows_to(j).start()

    def finish(k, carry):
        copy_to(k).wait_send()
        copy_from(k).wait_recv()
        return carry

    lax.fori_loop(1, n, finish, 0)
    local.wait()
    if with_rows:
        local2.wait()
        for j in range(1, n_row):
            rows_to(j).wait_send()
            rows_from(j).wait_recv()


def exchange(n_row, n_col, collective_id, send, extra=None):
    n = n_row * n_col
    with_rows = extra is not None
    args = (send, extra) if with_rows else (send,)
    sems = [pltpu.SemaphoreType.DMA, pltpu.SemaphoreType.DMA((n,)), pltpu.SemaphoreType.DMA((n,))]
    if with_rows:
        sems += [pltpu.SemaphoreType.DMA, pltpu.SemaphoreType.DMA((n_row,)), pltpu.SemaphoreType.DMA((n_row,))]
    return pl.pallas_call(
        functools.partial(exchange_kernel, n_row, n_col, with_rows),
        out_shape=tuple(jax.ShapeDtypeStruct(a.shape, a.dtype) for a in args),
        in_specs=[ANY] * len(args),
        out_specs=(ANY,) * len(args),
        scratch_shapes=sems,
        compiler_params=comm_params(collective_id),
        name="exchange",
    )(*args)


def gather_kernel(n_col, piece, out, local_sem, ssem, rsem):
    row, col = lax.axis_index("row"), lax.axis_index("col")
    n_x = n_col // 2
    x, k = col // 2, lax.rem(col, 2)
    right = lax.rem(x + 1, n_x) * 2 + k
    left = lax.rem(x + n_x - 1, n_x) * 2 + k
    far = lax.rem(x + 2, n_x) * 2 + k
    twin = x * 2 + 1 - k

    def other(c):
        return (c // 2) * 2 + 1 - k

    barrier = pltpu.get_barrier_semaphore()
    for c in (right, left, twin):
        pl.semaphore_signal(barrier, inc=1, device_id={"row": row, "col": c}, device_id_type=MESH)
    pl.semaphore_wait(barrier, 3)
    half = piece.shape[0] // 2
    low, high = pl.ds(0, half), pl.ds(half, half)

    def to(i, src, dst, c):
        return remote(src, dst, ssem.at[i], rsem.at[i], row=row, col=c)

    local = pltpu.make_async_copy(piece, out.at[col], local_sem)
    sends = [to(0, piece, out.at[col], right), to(1, piece, out.at[col], left), to(2, piece, out.at[col], twin)]
    for c in sends:
        c.start()
    local.start()

    def arrived(i, dst):
        to(i, dst, dst, col).wait_recv()

    def forward(i, src, c):
        copy = to(i, src, src, c)
        copy.start()
        sends.append(copy)

    arrived(0, out.at[left])
    forward(3, out.at[left, low], right)
    forward(4, out.at[left], twin)
    arrived(1, out.at[right])
    forward(5, out.at[right, high], left)
    forward(6, out.at[right], twin)
    arrived(3, out.at[far, low])
    forward(7, out.at[far, low], twin)
    arrived(5, out.at[far, high])
    forward(8, out.at[far, high], twin)
    arrived(2, out.at[twin])
    arrived(4, out.at[other(left)])
    arrived(6, out.at[other(right)])
    arrived(7, out.at[other(far), low])
    arrived(8, out.at[other(far), high])
    local.wait()
    for c in sends:
        c.wait_send()


def gather_cols(n_col, collective_id, piece):
    return pl.pallas_call(
        functools.partial(gather_kernel, n_col),
        out_shape=jax.ShapeDtypeStruct((n_col,) + piece.shape, piece.dtype),
        in_specs=[ANY],
        out_specs=ANY,
        scratch_shapes=[pltpu.SemaphoreType.DMA, pltpu.SemaphoreType.DMA((9,)), pltpu.SemaphoreType.DMA((9,))],
        compiler_params=comm_params(collective_id),
        name="gather_cols",
    )(piece)


def reduce_kernel(n_col, part, out, own, twin_part, from_far, from_near, local_sem, ssem, rsem):
    row, col = lax.axis_index("row"), lax.axis_index("col")
    n_x = n_col // 2
    x, k = col // 2, lax.rem(col, 2)
    xr, xl, xf = lax.rem(x + 1, n_x), lax.rem(x + n_x - 1, n_x), lax.rem(x + 2, n_x)
    right, left, twin = xr * 2 + k, xl * 2 + k, x * 2 + 1 - k
    barrier = pltpu.get_barrier_semaphore()
    for c in (right, left, twin):
        pl.semaphore_signal(barrier, inc=1, device_id={"row": row, "col": c}, device_id_type=MESH)
    pl.semaphore_wait(barrier, 3)
    rows = out.shape[0]
    half = rows // 2
    step = 16
    order = (xf, xr, xl, x)

    def to(i, src, dst, c):
        return remote(src, dst, ssem.at[i], rsem.at[i], row=row, col=c)

    sends, loads = [], []
    for j, xd in enumerate(order):
        sends.append(to(j, part.at[xd * 2 + 1 - k], twin_part.at[j], twin))
        loads.append(pltpu.make_async_copy(part.at[xd * 2 + k], own.at[j], local_sem.at[j]))
    for j in range(4):
        sends[j].start()
        loads[j].start()

    def add(dst, start, count, *srcs):
        def body(i, carry):
            at = pl.ds(pl.multiple_of(start + i * step, step), step)
            total = srcs[0][at, :].astype(jnp.float32)
            for s in srcs[1:]:
                total += s[at, :].astype(jnp.float32)
            dst[at, :] = total.astype(dst.dtype)
            return carry

        lax.fori_loop(0, count // step, body, 0)

    def arrived(i, dst):
        to(i, dst, dst, col).wait_recv()

    def send(i, src, dst, c):
        copy = to(i, src, dst, c)
        copy.start()
        sends.append(copy)

    low, high = pl.ds(0, half), pl.ds(half, half)
    for j in range(4):
        loads[j].wait()
        arrived(j, twin_part.at[j])
        if j == 0:
            add(own.at[0], 0, rows, own.at[0], twin_part.at[0])
            send(4, own.at[0, low], from_far.at[low], right)
            send(5, own.at[0, high], from_far.at[high], left)
        elif j == 1:
            arrived(4, from_far.at[low])
            add(own.at[1], 0, half, own.at[1], twin_part.at[1], from_far)
            add(own.at[1], half, half, own.at[1], twin_part.at[1])
            send(6, own.at[1], from_near.at[0], right)
        elif j == 2:
            arrived(5, from_far.at[high])
            add(own.at[2], half, half, own.at[2], twin_part.at[2], from_far)
            add(own.at[2], 0, half, own.at[2], twin_part.at[2])
            send(7, own.at[2], from_near.at[1], left)
        else:
            arrived(6, from_near.at[0])
            arrived(7, from_near.at[1])
            add(out, 0, rows, own.at[3], twin_part.at[3], from_near.at[0], from_near.at[1])
    for c in sends:
        c.wait_send()


def reduce_cols(n_col, collective_id, part):
    shape = part.shape[1:]
    return pl.pallas_call(
        functools.partial(reduce_kernel, n_col),
        out_shape=jax.ShapeDtypeStruct(shape, part.dtype),
        in_specs=[ANY],
        out_specs=pl.BlockSpec(memory_space=pltpu.VMEM),
        scratch_shapes=[
            pltpu.VMEM((4,) + shape, part.dtype),
            pltpu.VMEM((4,) + shape, part.dtype),
            pltpu.VMEM(shape, part.dtype),
            pltpu.VMEM((2,) + shape, part.dtype),
            pltpu.SemaphoreType.DMA((4,)),
            pltpu.SemaphoreType.DMA((8,)),
            pltpu.SemaphoreType.DMA((8,)),
        ],
        compiler_params=comm_params(collective_id, 40 * 2**20),
        name="reduce_cols",
    )(part)


def spread_kernel(n_col, piece, out, local_sem, ssem, rsem):
    row, col = lax.axis_index("row"), lax.axis_index("col")
    barrier = pltpu.get_barrier_semaphore()
    for j in range(1, n_col):
        pl.semaphore_signal(barrier, inc=1, device_id={"row": row, "col": lax.rem(col + j, n_col)}, device_id_type=MESH)
    pl.semaphore_wait(barrier, n_col - 1)
    local = pltpu.make_async_copy(piece, out.at[col], local_sem)
    local.start()
    sends = [remote(piece, out.at[col], ssem.at[j], rsem.at[j], row=row, col=lax.rem(col + j, n_col)) for j in range(1, n_col)]
    for c in sends:
        c.start()
    for j in range(1, n_col):
        source = lax.rem(col + n_col - j, n_col)
        remote(out.at[source], out.at[source], ssem.at[j], rsem.at[j], row=row, col=col).wait_recv()
    for c in sends:
        c.wait_send()
    local.wait()


def spread_cols(n_col, collective_id, piece):
    return pl.pallas_call(
        functools.partial(spread_kernel, n_col),
        out_shape=jax.ShapeDtypeStruct((n_col,) + piece.shape, piece.dtype),
        in_specs=[ANY],
        out_specs=ANY,
        scratch_shapes=[pltpu.SemaphoreType.DMA, pltpu.SemaphoreType.DMA((n_col,)), pltpu.SemaphoreType.DMA((n_col,))],
        compiler_params=comm_params(collective_id),
        name="spread_cols",
    )(piece)


def solution(mesh):
    row_size = mesh.shape["row"]
    col_size = mesh.shape["col"]
    group = row_size * col_size
    act_spec = P("dp", None, ("row", "col"))
    weight_spec = P(None, "row", "col")

    def device_fn(x_loc, gain_loc, w_in_loc, w_kv_loc, w_out_loc):
        n_layers = w_in_loc.shape[0]
        n_batch, seq_len, d_local = x_loc.shape
        d_model = d_local * group
        e_block = w_in_loc.shape[2]
        r_block = w_out_loc.shape[1]
        f_block = e_block - r_block
        f_half = f_block // 2
        q_block = r_block - f_block
        kv_local = w_kv_loc.shape[2]
        head_dim = kv_local * col_size // 2
        heads_local = q_block // head_dim
        n_tok = n_batch * seq_len
        tok_loc = n_tok // group
        tok_row = n_tok // row_size
        seqs = n_batch // row_size
        seq_local = seq_len // group
        cos_tab, sin_tab = rope_tables(jnp.arange(seq_len), head_dim)
        causal = jnp.arange(seq_len)[None, :] <= jnp.arange(seq_len)[:, None]

        w_a, w_b, w_o = [], [], []
        for l in range(n_layers):
            gate_up = w_in_loc[l, :, q_block:]
            first = jnp.concatenate([gate_up[:, :f_half], gate_up[:, f_block : f_block + f_half], w_in_loc[l, :, :q_block], w_kv_loc[l]], axis=1)
            second = jnp.concatenate([gate_up[:, f_half:f_block], gate_up[:, f_block + f_half :]], axis=1)
            w_a.append(lax.all_gather(first, "row", axis=0, tiled=True))
            w_b.append(lax.all_gather(second, "row", axis=0, tiled=True))
            w_o.append(lax.all_gather(w_out_loc[l], "row", axis=0))

        pieces = x_loc.reshape(group, tok_loc, d_local).transpose(0, 2, 1)
        gain_rows = jnp.pad(gain_loc, ((0, 16 - n_layers), (0, tok_loc - d_local)))
        pieces = jnp.concatenate([pieces, jnp.broadcast_to(gain_rows[None], (group,) + gain_rows.shape)], axis=1)
        (got,) = exchange(row_size, col_size, 0, pieces)
        hidden = got[:, :d_local].reshape(d_model, tok_loc).T
        gain = got[:, d_local : d_local + n_layers, :d_local].transpose(1, 0, 2).reshape(n_layers, d_model)

        kv_rows = []
        for l in range(n_layers):
            hidden_f32 = hidden.astype(jnp.float32)
            centered = hidden_f32 - jnp.mean(hidden_f32, axis=-1, keepdims=True)
            variance = jnp.mean(centered * centered, axis=-1, keepdims=True)
            normed = (centered * lax.rsqrt(variance + LN_EPS) * gain[l].astype(jnp.float32)).astype(jnp.bfloat16)
            normed_row = gather_cols(col_size, 1 + 4 * l, normed).reshape(tok_row, d_model)
            proj_a = jnp.dot(normed_row, w_a[l], preferred_element_type=jnp.float32).astype(jnp.bfloat16)
            kv_piece = jnp.pad(proj_a[:, f_block + q_block :].T, ((0, 32 - kv_local), (0, 0)))
            kv_all = spread_cols(col_size, 2 + 4 * l, kv_piece)[:, :kv_local].reshape(2, head_dim, seqs, seq_len)
            proj_b = jnp.dot(normed_row, w_b[l], preferred_element_type=jnp.float32).astype(jnp.bfloat16)
            key, v_val = (a.transpose(1, 2, 0) for a in (kv_all[0], kv_all[1]))
            query = proj_a[:, f_block : f_block + q_block].reshape(seqs, seq_len, heads_local, head_dim)
            q_rot = (apply_rope(query.astype(jnp.float32), cos_tab[:, None, :], sin_tab[:, None, :]) * head_dim ** -0.5).astype(jnp.bfloat16)
            k_rot = apply_rope(key.astype(jnp.float32), cos_tab, sin_tab).astype(jnp.bfloat16)
            scores = jnp.einsum("crie,cle->cirl", q_rot, k_rot, preferred_element_type=jnp.float32)
            scores = jnp.where(causal, scores, -1e30)
            attn_prob = jax.nn.softmax(scores, axis=-1).astype(jnp.bfloat16)
            attn_out = jnp.einsum("cirl,cle->crie", attn_prob, v_val, preferred_element_type=jnp.float32).astype(jnp.bfloat16).reshape(tok_row, q_block)

            def swish_mul(gate_val, up_val):
                return (jax.nn.silu(gate_val.astype(jnp.float32)) * up_val.astype(jnp.float32)).astype(jnp.bfloat16)

            joined = jnp.concatenate(
                [attn_out, swish_mul(proj_a[:, :f_half], proj_a[:, f_half:f_block]), swish_mul(proj_b[:, :f_half], proj_b[:, f_half:])], axis=1
            )
            part_out = jnp.einsum("tk,rkn->trn", joined, w_o[l], preferred_element_type=jnp.float32).astype(jnp.bfloat16)
            update = reduce_cols(col_size, 3 + 4 * l, part_out.reshape(col_size, tok_loc, d_model))
            hidden = hidden + update
            kv_rows.append(jnp.stack([k_rot, v_val]))

        col = lax.axis_index("col")
        kv_rows = jnp.stack(kv_rows).reshape(n_layers, 2, seqs, row_size, col_size, seq_local, head_dim)
        kv_mine = lax.dynamic_index_in_dim(kv_rows, col, axis=4, keepdims=False)
        kv_send = kv_mine.transpose(3, 5, 0, 1, 2, 4).reshape(row_size, head_dim, n_layers * 2 * seqs * seq_local)
        out_pieces, kv_got = exchange(row_size, col_size, 15, hidden.T.reshape(group, d_local, tok_loc), kv_send)
        y_out = out_pieces.transpose(0, 2, 1).reshape(n_batch, seq_len, d_local)
        kv_out = kv_got.reshape(row_size, head_dim, n_layers, 2, seqs, seq_local).transpose(2, 3, 0, 4, 5, 1)
        return y_out, kv_out.reshape(n_layers, 2, n_batch, seq_local, head_dim)

    return jax.shard_map(device_fn, mesh=mesh, in_specs=(act_spec, P(None, ("row", "col")), weight_spec, weight_spec, P(None, "col", "row")), out_specs=(act_spec, P(None, None, "dp", ("row", "col"), None)), check_vma=False)
```

time: 2360 us -> 773 us (0.33)
  waiting for transfers between devices: 1790 us -> 40.3 us
  Pallas kernels: 0 us -> 299 us
  local copies, waits for them, and re-layouts: 18.6 us -> 206 us
  blocking collectives: 183 us -> 0 us
  matrix products: 259 us -> 166 us
  other arithmetic: 88.5 us -> 41.5 us
    psum x2 -> x0, waiting for transfers between devices: 1570 us -> none  [device_fn(): main_proj, kv_piece = lax.psum((part_main, part_kv), 'row')]
    pallas_call x0 -> x8, Pallas kernels: none -> 299 us  [the longest x2 104 us: reduce_cols(): pl.pallas_call(functools.partial(reduce_kernel, n_col), out_shape=jax.Sha...]
    psum x4 -> x0, blocking collectives: 183 us -> none  [the longest x2 95.7 us: device_fn(): lax.psum(jnp.sum(hidden_f32, axis=-1, keepdims=True), ('row', 'col'))]
    convert_element_type x0 -> x12, local copies, waits for them, and re-layouts: none -> 117 us  [the longest x2 105 us: device_fn(): jnp.einsum('tk,rkn->trn', joined, w_o[l], preferred_element_type=jnp.floa...]
    reduce_scatter x2 -> x0, waiting for transfers between devices: 112 us -> none  [device_fn(): update = lax.psum_scatter(part_out, 'col', scatter_dimension=2, tiled=True)]
    all_gather x4 -> x6, waiting for transfers between devices: 108 us -> 39.5 us  [the longest x2 36.3 us: device_fn(): w_a.append(lax.all_gather(first, 'row', axis=0, tiled=True))]
    dot_general x2, matrix products: 62.3 us -> 14.9 us  [device_fn(): jnp.einsum('cirl,cle->crie', attn_prob, v_val, preferred_element_type=jnp...]
    convert_element_type x7, other arithmetic: 59.8 us -> 14.1 us  [the longest x4 10.9 us: swish_mul(): (jax.nn.silu(gate_val.astype(jnp.float32)) * up_val.astype(jnp.float32))....]
  transfers between devices with their start and end apart: 8 -> 6, of which waited for: 6 -> 2; matrix products, arithmetic and copies ran while one was open for 3% -> 38% of each run, Pallas kernels for 0% -> 29%
where the time goes in v1:
time: 773 us; the launch traced here: 768 us
  Pallas kernels  299 us (39%)
  local copies, waits for them, and re-layouts  206 us (27%)
  matrix products  166 us (21%)
  other arithmetic  41.5 us (5%)
  waiting for transfers between devices  40.3 us (5%)
  between operations  14.9 us (2%)
    convert_element_type x2, local copies, waits for them, and re-layouts, device_fn(): jnp.einsum('tk,rkn->trn', joined, w_o[l], preferred_element_type=jnp.floa...  105 us
    pallas_call x2, Pallas kernels, reduce_cols(): pl.pallas_call(functools.partial(reduce_kernel, n_col), out_shape=jax.Sha...  104 us
    pallas_call x2, Pallas kernels, gather_cols(): pl.pallas_call(functools.partial(gather_kernel, n_col), out_shape=jax.Sha...  101 us
    pallas_call x2, Pallas kernels, exchange(): pl.pallas_call(functools.partial(exchange_kernel, n_row, n_col, with_rows...  61.1 us
    dot_general x2, matrix products, device_fn(): jnp.einsum('tk,rkn->trn', joined, w_o[l], preferred_element_type=jnp.floa...  47.5 us
    dot_general x2, matrix products, device_fn(): jnp.dot(normed_row, w_a[l], preferred_element_type=jnp.float32)  46.4 us
    all_gather x2, waiting for transfers between devices, device_fn(): w_a.append(lax.all_gather(first, 'row', axis=0, tiled=True))  36.3 us
    dot_general x2, matrix products, device_fn(): jnp.dot(normed_row, w_b[l], preferred_element_type=jnp.float32)  36.2 us
  transfers between devices with their start and end apart: 6, of which 2 were waited for; matrix products, arithmetic and copies ran while one was open for 38% of the time, Pallas kernels for 29%

profile of v1, /device:TPU:97, one launch (start us, length us, event | category | flops | bytes accessed | tf_op | source)
XLA Modules:
  0.0 767.5 jit_solution(2821680514262592499)
XLA Ops:
  7.2 3.5 slice_bitcast_fusion
  19.1 4.5 fusion.112
  32.7 33.4 %exchange.2 = bf16[32,96,256]{2,1,0:T(8,128)(2,1)} custom-call(bf16[32,96,256]{2,1,0:T(8,128)(2,1)} %pad_maximum_fusion.4.refs_0_), custom_call_target="tpu_custom_call" | custom-call | tf_op jit(solution)/shard_map/exchange/pallas_call | solution.py:106
  72.4 50.6 %gather_cols.2 = bf16[8,256,2560]{2,1,0:T(8,128)(2,1)} custom-call(bf16[256,2560]{1,0:T(8,128)(2,1)} %fusion.51.piece), custom_call_target="tpu_custom_call" | custom-call | tf_op jit(solution)/shard_map/gather_cols/pallas_call | solution.py:174
  124.7 18.1 %convolution_convert_fusion.3 = bf16[2048,1280]{0,1:T(8,128)(2,1)S(1)} fusion(bf16[2048,2560]{1,0:T(8,128)(2,1)} %bitcast.169, bf16[2560,1280]{0,1:T(8,128)(2,1)} %all-gather.9.cloned.1.call-done), kind=kOutput, calls=%fused_computation.19 | convolution fusion | flops 13424394240 | bytes 22282240 | tf_op jit(solution)/shard_map/dot_general | solution.py:361
  145.7 36.3 %all-gather.7.cloned.1.call-done = bf16[2560,1620]{0,1:T(8,128)(2,1)} async-done(((bf16[640,1620]{0,1:T(8,128)(2,1)}), bf16[2560,1620]{0,1:T(8,128)(2,1)}) %all-gather.7.cloned.1.call-update) | async-done | bytes 8294416 | tf_op jit(solution)/shard_map/all_gather | solution.py:340
  182.0 22.4 %convolution_convert_fusion.1 = bf16[2048,1620]{0,1:T(8,128)(2,1)S(1)} fusion(bf16[2048,2560]{1,0:T(8,128)(2,1)} %bitcast.170, bf16[2560,1620]{0,1:T(8,128)(2,1)} %all-gather.7.cloned.1.call-done), kind=kOutput, calls=%fused_computation.17 | convolution fusion | flops 16990248960 | bytes 25415680 | tf_op jit(solution)/shard_map/dot_general | solution.py:358
  204.4 3.3 fusion.41
  208.8 17.0 %spread_cols.2 = bf16[8,32,2048]{2,1,0:T(8,128)(2,1)} custom-call(bf16[32,2048]{1,0:T(8,128)(2,1)} %pad.12.piece), custom_call_target="tpu_custom_call" | custom-call | tf_op jit(solution)/shard_map/spread_cols/pallas_call | solution.py:297
  240.6 10.1 %fusion.120 = (f32[4,4,512]{2,1,0:T(4,128)S(1)}, f32[4,4,512,512]{2,3,1,0:T(8,128)}) fusion(pred[512,512]{0,1:T(8,128)(4,1)} %iota_compare_fusion, bf16[4,512,40]{1,2,0:T(8,128)(2,1)S(1)} %copy-done.17, bf16[4,512,40]{1,2,0:T(8,128)(2,1)S(1)} %copy-done.16, f32[4,512,4,40]{1,3,2,0:T(8,128)} %get-tuple-element.33, f32[4,512,4,40]{1,3,2,0:T(8,128)} %get-tuple-element.32), kind=kOutput, calls=%fused_computation.174 | convolution fusion | flops 686293504 | bytes 20021248 | tf_op jit(solution)/shard_map/sub | solution.py:368
  250.7 7.4 fusion.60
  260.5 3.1 all-gather.11.cloned.1.call-done
  263.7 23.9 %fusion.21 = bf16[2048,4,640]{2,0,1:T(8,128)(2,1)S(1)} fusion(bf16[4,1600,640]{2,1,0:T(8,128)(2,1)} %all-gather.11.cloned.1.call-done, bf16[2048,640]{0,1:T(8,128)(2,1)S(1)} %copy-done.6, bf16[2048,640]{0,1:T(8,128)(2,1)} %fusion.41, bf16[2048,320]{0,1:T(8,128)(2,1)} %bitcast.187), kind=kOutput, calls=%fused_computation.41 | convolution fusion | flops 16802119680 | bytes 25231360 | tf_op jit(solution)/shard_map/tk,rkn->trn/dot_general | solution.py:377
  287.5 52.5 %copy.97 = bf16[2048,4,640]{2,1,0:T(4,128)(2,1)} copy(bf16[2048,4,640]{2,0,1:T(8,128)(2,1)S(1)} %fusion.21) | data formatting | bytes 20971520 | tf_op jit(solution)/shard_map/convert_element_type | solution.py:377
  340.0 17.6 %reshape.314.part = bf16[8,256,2560]{2,1,0:T(8,128)(2,1)} reshape(bf16[2048,4,640]{2,1,0:T(4,128)(2,1)} %copy.97) | data formatting | bytes 20971520 | tf_op jit(solution)/shard_map/reshape | solution.py:378
  357.6 4.0 copy-done
  361.6 54.3 %reduce_cols.2 = bf16[256,2560]{1,0:T(8,128)(2,1)S(1)} custom-call(bf16[8,256,2560]{2,1,0:T(8,128)(2,1)S(1)} %copy-done), custom_call_target="tpu_custom_call" | custom-call | tf_op jit(solution)/shard_map/reduce_cols/pallas_call | solution.py:258
  419.0 50.1 %gather_cols.3 = bf16[8,256,2560]{2,1,0:T(8,128)(2,1)} custom-call(bf16[256,2560]{1,0:T(8,128)(2,1)} %fusion.48.piece), custom_call_target="tpu_custom_call" | custom-call | tf_op jit(solution)/shard_map/gather_cols/pallas_call | solution.py:174
  469.1 24.0 %convolution_convert_fusion = bf16[2048,1620]{0,1:T(8,128)(2,1)} fusion(bf16[2048,2560]{1,0:T(8,128)(2,1)} %bitcast.167, bf16[2560,1620]{0,1:T(8,128)(2,1)} %all-gather.13.cloned.1.call-done), kind=kOutput, calls=%fused_computation.16 | convolution fusion | flops 16990248960 | bytes 25415680 | tf_op jit(solution)/shard_map/dot_general | solution.py:358
  497.8 15.8 %spread_cols.3 = bf16[8,32,2048]{2,1,0:T(8,128)(2,1)} custom-call(bf16[32,2048]{1,0:T(8,128)(2,1)} %pad.13.piece), custom_call_target="tpu_custom_call" | custom-call | tf_op jit(solution)/shard_map/spread_cols/pallas_call | solution.py:297
  516.2 3.2 slice_convert_fusion
  519.4 3.4 reshape.326
  533.1 10.6 %fusion.125 = (f32[4,4,512]{2,1,0:T(4,128)S(1)}, f32[4,4,512,512]{2,3,1,0:T(8,128)}) fusion(pred[512,512]{0,1:T(8,128)(4,1)S(1)} %copy-done.20, bf16[4,512,40]{1,2,0:T(8,128)(2,1)S(1)} %copy-done.19, bf16[4,512,40]{1,2,0:T(8,128)(2,1)S(1)} %copy-done.18, f32[4,512,4,40]{1,3,2,0:T(8,128)} %get-tuple-element.31, f32[4,512,4,40]{1,3,2,0:T(8,128)S(1)} %get-tuple-element.30), kind=kOutput, calls=%fused_computation.175 | convolution fusion | flops 686293504 | bytes 20021248 | tf_op jit(solution)/shard_map/sub | solution.py:368
  543.7 7.5 fusion.61
  555.5 18.1 %convolution_convert_fusion.2 = bf16[2048,1280]{0,1:T(8,128)(2,1)S(1)} fusion(bf16[2048,2560]{1,0:T(8,128)(2,1)} %bitcast.168, bf16[2560,1280]{0,1:T(8,128)(2,1)} %all-gather.15.cloned.1.call-done), kind=kOutput, calls=%fused_computation.18 | convolution fusion | flops 13424394240 | bytes 22282240 | tf_op jit(solution)/shard_map/dot_general | solution.py:361
  573.6 2.9 fusion.38
  576.6 23.7 %fusion.20 = bf16[2048,4,640]{2,0,1:T(8,128)(2,1)S(1)} fusion(bf16[4,1600,640]{2,1,0:T(8,128)(2,1)} %all-gather.17.cloned.1.call-done, bf16[2048,640]{0,1:T(8,128)(2,1)} %fusion.38, bf16[2048,640]{0,1:T(8,128)(2,1)S(1)} %fusion.39, bf16[2048,320]{0,1:T(8,128)(2,1)} %bitcast.186), kind=kOutput, calls=%fused_computation.40 | convolution fusion | flops 16802119680 | bytes 25231360 | tf_op jit(solution)/shard_map/tk,rkn->trn/dot_general | solution.py:377
  600.2 52.6 %copy.105 = bf16[2048,4,640]{2,1,0:T(4,128)(2,1)} copy(bf16[2048,4,640]{2,0,1:T(8,128)(2,1)S(1)} %fusion.20) | data formatting | bytes 20971520 | tf_op jit(solution)/shard_map/convert_element_type | solution.py:377
  652.9 17.7 %reshape.317.part = bf16[8,256,2560]{2,1,0:T(8,128)(2,1)} reshape(bf16[2048,4,640]{2,1,0:T(4,128)(2,1)} %copy.105) | data formatting | bytes 20971520 | tf_op jit(solution)/shard_map/reshape | solution.py:378
  670.5 4.0 copy-done.1
  674.5 49.8 %reduce_cols.3 = bf16[256,2560]{1,0:T(8,128)(2,1)S(1)} custom-call(bf16[8,256,2560]{2,1,0:T(8,128)(2,1)S(1)} %copy-done.1), custom_call_target="tpu_custom_call" | custom-call | tf_op jit(solution)/shard_map/reduce_cols/pallas_call | solution.py:258
  727.8 27.7 %exchange.3 = (bf16[32,80,256]{2,1,0:T(8,128)(2,1)}, bf16[4,80,256]{2,1,0:T(8,128)(2,1)}) custom-call(bf16[32,80,256]{2,1,0:T(8,128)(2,1)} %bitcast.173, bf16[4,80,256]{2,1,0:T(8,128)(2,1)} %copy.114.refs_1_), custom_call_target="tpu_custom_call" | custom-call | tf_op jit(solution)/shard_map/exchange/pallas_call | solution.py:106
  (146 shorter events, 79.7 us)
Async XLA Ops:
  7.2 117.5 %all-gather.9.cloned.1.call-start = ((), (), s32[]{:S(2)}) async-start(), calls=%async_computation.1 | async-start | bytes 8192000 | tf_op jit(solution)/shard_map/all_gather | solution.py:341
  12.5 1.5 copy-start.21
  13.9 168.1 %all-gather.7.cloned.1.call-start = ((), (), s32[]{:S(2)}) async-start(), calls=%async_computation | async-start | bytes 10393600 | tf_op jit(solution)/shard_map/all_gather | solution.py:340
  19.0 244.6 %all-gather.11.cloned.1.call-start = ((), (), s32[]{:S(2)}) async-start(), calls=%async_computation.2 | async-start | bytes 10240000 | tf_op jit(solution)/shard_map/all_gather | solution.py:342
  23.6 445.5 %all-gather.13.cloned.1.call-start = ((), (), s32[]{:S(2)}) async-start(), calls=%async_computation.3 | async-start | bytes 10393600 | tf_op jit(solution)/shard_map/all_gather | solution.py:340
  26.3 529.2 %all-gather.15.cloned.1.call-start = ((), (), s32[]{:S(2)}) async-start(), calls=%async_computation.4 | async-start | bytes 8192000 | tf_op jit(solution)/shard_map/all_gather | solution.py:341
  27.7 1.3 copy-start.13
  27.8 548.8 %all-gather.17.cloned.1.call-start = ((), (), s32[]{:S(2)}) async-start(), calls=%async_computation.5 | async-start | bytes 10240000 | tf_op jit(solution)/shard_map/all_gather | solution.py:342
  29.8 1.5 copy-start.24
  70.0 2.5 copy-start.2
  124.7 113.6 %copy-start.9 = (f32[512,40]{0,1:T(8,128)}, f32[512,40]{0,1:T(8,128)S(1)}, u32[]{:S(2)}) copy-start(f32[512,40]{0,1:T(8,128)S(1)} %get-tuple-element.48) | copy-start | bytes 245764
  233.2 4.3 copy-start.11
  238.3 2.3 copy-start.16
  238.3 2.3 copy-start.17
  240.6 10.1 %copy-start.14 = (bf16[80,4,512]{2,1,0:T(4,128)(2,1)S(1)}, bf16[80,4,512]{2,1,0:T(4,128)(2,1)}, u32[]{:S(2)}) copy-start(bf16[80,4,512]{2,1,0:T(4,128)(2,1)} %squeeze.35) | copy-start | bytes 983044
  258.1 5.6 copy-start.6
  357.6 4.0 copy-start
  361.6 54.3 %copy-start.3 = (bf16[2560,256]{0,1:T(8,128)(2,1)S(1)}, bf16[2560,256]{0,1:T(8,128)(2,1)}, u32[]{:S(2)}) copy-start(bf16[2560,256]{0,1:T(8,128)(2,1)} %copy-done.2) | copy-start | bytes 3932164
  415.9 1.6 copy-start.23
  519.4 7.4 copy-start.10
  519.4 7.4 copy-start.12
  531.2 1.9 copy-start.18
  531.2 1.9 copy-start.19
  531.2 1.9 copy-start.20
  533.1 10.6 %copy-start.15 = (bf16[80,4,512]{2,1,0:T(4,128)(2,1)S(1)}, bf16[80,4,512]{2,1,0:T(4,128)(2,1)}, u32[]{:S(2)}) copy-start(bf16[80,4,512]{2,1,0:T(4,128)(2,1)} %squeeze.39) | copy-start | bytes 983044
  543.7 10.0 %slice-start = ((s8[6651904]{0:T(1024)(128)(4,1)}), s8[4194304]{0:T(1024)(128)(4,1)S(1)}, s32[]{:S(2)}) async-start(s8[6651904]{0:T(1024)(128)(4,1)} %bitcast.171), calls=%async_computation.6 | async-start | bytes 8388608
  543.7 10.0 %slice-start.1 = ((s8[6651904]{0:T(1024)(128)(4,1)}), s8[2457600]{0:T(1024)(128)(4,1)S(1)}, s32[]{:S(2)}) async-start(s8[6651904]{0:T(1024)(128)(4,1)} %bitcast.171), calls=%async_computation.7 | async-start | bytes 4915200
  670.5 4.0 copy-start.1
  674.5 49.8 %copy-start.5 = (bf16[256,2560]{1,0:T(8,128)(2,1)S(1)}, bf16[256,2560]{1,0:T(8,128)(2,1)}, u32[]{:S(2)}) copy-start(bf16[256,2560]{1,0:T(8,128)(2,1)} %copy-done.4) | copy-start | bytes 3932164
  724.3 1.6 copy-start.7
  724.3 1.6 copy-start.8
  757.3 2.3 copy-start.22
  (1 other events, 1.1 us)
Sparse Core Ops, SparseCore 0:
  14.1 84.1 all-gather.8
  99.9 82.0 all-gather.6
  183.6 80.0 all-gather.10
  265.1 81.0 all-gather.12
  347.6 66.2 all-gather.14
  415.4 79.8 all-gather.16

commit v2 on v0

v2 whole, which is shorter than its diff:
```python
import functools

import numpy as np

import jax
import jax.numpy as jnp
from jax import lax
from jax.experimental import pallas as pl
from jax.experimental.pallas import tpu as pltpu
from jax.sharding import PartitionSpec as P

LN_EPS = 1e-6
MESH = pl.DeviceIdType.MESH
ANY = pl.BlockSpec(memory_space=pl.ANY)
VMEM = pl.BlockSpec(memory_space=pltpu.VMEM)
F32, BF16 = jnp.float32, jnp.bfloat16
SLOTS = 6
AHEAD = 4


def dot(a, b):
    return jnp.dot(a, b, preferred_element_type=F32)


class Dims:
    pass


def kernel(
    D,
    x_t, gains, w_t, wkv_t, wo_t, cos_ref, sin_ref, perm_ref,
    y_out, kv_out, g_w, g_kv, g_wo,
    xland, gland, gcol, hid, ht, wbuf, wobuf, qt, kvland, kn, vt, kvbuf, jt, ot, twin_in, far_in, near_in,
    xs, xr, gs, gr, ys, yr, ags, agr, kvs, kvr, rss, rsr, lsem, fs, fr, fl,
):
    row, col = lax.axis_index("row"), lax.axis_index("col")
    n_row, n_col, n = D.n_row, D.n_col, D.n_row * D.n_col
    n_x = n_col // 2
    me = row * n_col + col
    x, k = col // 2, lax.rem(col, 2)
    xr_, xl_, xf_ = lax.rem(x + 1, n_x), lax.rem(x + n_x - 1, n_x), lax.rem(x + 2, n_x)
    right, left, twin = xr_ * 2 + k, xl_ * 2 + k, x * 2 + 1 - k
    up, down, across = lax.rem(row + 1, n_row), lax.rem(row + n_row - 1, n_row), lax.rem(row + 2, n_row)
    tok, dl, dr = D.tok, D.dl, D.dr
    my_lanes = pl.ds(pl.multiple_of(k * tok, 128), tok)
    twin_lanes = pl.ds(pl.multiple_of((1 - k) * tok, 128), tok)

    def remote(src, dst, ssem, rsem, r, c):
        return pltpu.make_async_remote_copy(src_ref=src, dst_ref=dst, send_sem=ssem, recv_sem=rsem, device_id={"row": r, "col": c}, device_id_type=MESH)

    barrier = pltpu.get_barrier_semaphore()

    def greet(i, carry):
        d = lax.rem(me + i, n)
        pl.semaphore_signal(barrier, inc=1, device_id={"row": d // n_col, "col": lax.rem(d, n_col)}, device_id_type=MESH)
        return carry

    lax.fori_loop(1, n, greet, 0)
    pl.semaphore_wait(barrier, n - 1)

    def piece_of(ref, d):
        return ref.at[d // 2, :, pl.ds(pl.multiple_of(lax.rem(d, 2) * tok, 128), tok)]

    def x_copy(i):
        d = lax.rem(me + i, n)
        return remote(piece_of(x_t, d), xland.at[me], xs.at[i], xr.at[i], d // n_col, lax.rem(d, n_col))

    def g_copy(i):
        d = lax.rem(me + i, n)
        return remote(gains, gland.at[me], gs.at[i], gr.at[i], d // n_col, lax.rem(d, n_col))

    def x_start(i, carry):
        x_copy(i).start()
        g_copy(i).start()
        return carry

    own_x = pltpu.make_async_copy(piece_of(x_t, me), xland.at[me], xr.at[0])
    own_g = pltpu.make_async_copy(gains, gland.at[me], gr.at[0])
    own_x.start()
    own_g.start()
    lax.fori_loop(1, n, x_start, 0)

    def own_lanes(r):
        return pl.ds(pl.multiple_of(r * dr, 128), dr)

    half_q, fch, och = D.q // 2, D.fch, D.och

    def parts(t):
        l, s = t // D.steps, t % D.steps
        out = []

        def w_rows(a, m):
            out.append((w_t.at[l, pl.ds(a, m), :], lambda r, a=a, m=m: g_w.at[l, pl.ds(a, m), own_lanes(r)]))

        if s == 0:
            w_rows(0, half_q)
            w_rows(half_q, half_q)
            for a in (0, D.kvp // 2):
                out.append((wkv_t.at[l, pl.ds(a, D.kvp // 2), :], lambda r, a=a: g_kv.at[l, pl.ds(a, D.kvp // 2), own_lanes(r)]))
        elif s <= D.n_f:
            w_rows(D.q + (s - 1) * fch, fch)
            w_rows(D.q + D.f + (s - 1) * fch, fch)
        else:
            h = och // 2
            for a in ((s - 1 - D.n_f) * och, (s - 1 - D.n_f) * och + h):
                out.append((wo_t.at[l, pl.ds(a, h), :], lambda r, a=a: g_wo.at[l, r, pl.ds(a, h), :]))
        return out

    n_steps = D.layers * D.steps
    pending = {}

    def y_copy(t, i, kind, src, dst, r):
        return remote(src, dst, ys.at[t % SLOTS, i, kind], yr.at[t % SLOTS, i, kind], r, col)

    def drain(t):
        for c in pending.pop(t, ()):
            c.wait_send()

    def issue(t):
        if t >= n_steps:
            return
        drain(t - SLOTS)
        pending[t] = []
        for i, (src, place) in enumerate(parts(t)):
            for kind, r in ((0, up), (1, down)):
                c = y_copy(t, i, kind, src, place(row), r)
                c.start()
                pending[t].append(c)

    def relay(t):
        if t >= n_steps:
            return
        for i, (src, place) in enumerate(parts(t)):
            for kind, r, to in ((0, down, up), (1, up, down)):
                y_copy(t, i, kind, src, place(r), r).wait_recv()
                if kind == i % 2:
                    c = y_copy(t, i, 2, place(r), place(r), to)
                    c.start()
                    pending[t].append(c)

    y_next = [0]

    def advance():
        t = y_next[0]
        if t >= n_steps:
            return
        for i, (src, place) in enumerate(parts(t)):
            y_copy(t, i, 2, src, place(across), across).wait_recv()
        relay(t + 1)
        issue(t + AHEAD)
        y_next[0] = t + 1

    for t in range(AHEAD):
        issue(t)

    loaded = {}

    def load(t):
        if t in loaded or t >= n_steps:
            return
        while y_next[0] <= t:
            advance()
        l, s = t // D.steps, t % D.steps
        slot = t % 2
        copies = []

        def fetch(src, dst):
            c = pltpu.make_async_copy(src, dst, lsem.at[slot, len(copies)])
            c.start()
            copies.append(c)

        def w_rows(a, m, at):
            fetch(w_t.at[l, pl.ds(a, m), :], wbuf.at[slot, pl.ds(at, m), own_lanes(row)])
            for r in (up, down, across):
                fetch(g_w.at[l, pl.ds(a, m), own_lanes(r)], wbuf.at[slot, pl.ds(at, m), own_lanes(r)])

        if s == 0:
            w_rows(0, D.q, 0)
            kv_rows = pl.ds(D.q, D.kvp)
            fetch(wkv_t.at[l], wbuf.at[slot, kv_rows, own_lanes(row)])
            for r in (up, down, across):
                fetch(g_kv.at[l, :, own_lanes(r)], wbuf.at[slot, kv_rows, own_lanes(r)])
        elif s <= D.n_f:
            w_rows(D.q + (s - 1) * fch, fch, 0)
            w_rows(D.q + D.f + (s - 1) * fch, fch, fch)
        else:
            a = (s - 1 - D.n_f) * och
            at = lambda r: pl.ds(pl.multiple_of(r * och, 128), och)
            fetch(wo_t.at[l, pl.ds(a, och), :], wobuf.at[slot, at(row), :])
            for r in (up, down, across):
                fetch(g_wo.at[l, r, pl.ds(a, och), :], wobuf.at[slot, at(r), :])
        loaded[t] = copies

    def use(t):
        load(t)
        for c in loaded[t]:
            c.wait()
        if t + 1 < n_steps and y_next[0] > t + 1:
            load(t + 1)
        return t % 2

    own_x.wait()
    own_g.wait()

    def x_finish(i, carry):
        s = lax.rem(me + n - i, n)
        remote(xland.at[s], xland.at[s], xs.at[i], xr.at[i], row, col).wait_recv()
        remote(gland.at[s], gland.at[s], gs.at[i], gr.at[i], row, col).wait_recv()
        x_copy(i).wait_send()
        g_copy(i).wait_send()
        return carry

    lax.fori_loop(1, n, x_finish, 0)

    relay(0)

    def keep(d, carry):
        hid[pl.ds(pl.multiple_of(d * dl, 16), dl), :] = xland[d]
        return carry

    lax.fori_loop(0, n, keep, 0)
    g_all = gland[...].astype(F32)
    for l in range(D.layers):
        g_rows = g_all[:, l, :]
        g_rows = jnp.concatenate([g_rows, jnp.zeros((128 - n, 128), F32)], axis=0) if n < 128 else g_rows
        g_cols = g_rows.T
        for d in range(n):
            gcol[l, d * dl : (d + 1) * dl, :] = jnp.broadcast_to(g_cols[:dl, d : d + 1], (dl, 128))

    blk = 64
    n_blk = D.d // blk

    def layer_norm(l):
        def add_up(i, acc):
            v = hid[pl.ds(pl.multiple_of(i * blk, blk), blk), :].astype(F32)
            return acc + v.reshape(blk // 8, 8, tok).sum(axis=0)

        mean = lax.fori_loop(0, n_blk, add_up, jnp.zeros((8, tok), F32)).sum(axis=0, keepdims=True) / D.d

        def add_sq(i, acc):
            v = hid[pl.ds(pl.multiple_of(i * blk, blk), blk), :].astype(F32) - mean
            return acc + (v * v).reshape(blk // 8, 8, tok).sum(axis=0)

        var = lax.fori_loop(0, n_blk, add_sq, jnp.zeros((8, tok), F32)).sum(axis=0, keepdims=True) / D.d
        scale = lax.rsqrt(var + LN_EPS)

        def write(i, carry):
            rows = pl.ds(pl.multiple_of(i * blk, blk), blk)
            g = gcol[l, rows, :]
            g = jnp.concatenate([g] * (tok // 128), axis=1)
            v = (hid[rows, :].astype(F32) - mean) * scale * g
            ht[x, rows, my_lanes] = v.astype(BF16)
            return carry

        lax.fori_loop(0, n_blk, write, 0)

    d_low, d_high = pl.ds(0, D.d // 2), pl.ds(D.d // 2, D.d // 2)
    every = slice(None)

    class Gather:
        def __init__(self):
            self.sends = []
            mine = ht.at[x, :, my_lanes]
            for i, c in ((0, right), (1, left), (2, twin)):
                self.send(i, mine, c)

        def send(self, i, ref, c):
            copy = remote(ref, ref, ags.at[i], agr.at[i], row, c)
            copy.start()
            self.sends.append(copy)

        def arrived(self, i, ref):
            remote(ref, ref, ags.at[i], agr.at[i], row, col).wait_recv()

        def pass_on(self):
            self.arrived(0, ht.at[xl_, :, my_lanes])
            self.send(3, ht.at[xl_, d_low, my_lanes], right)
            self.send(4, ht.at[xl_, :, my_lanes], twin)
            self.arrived(1, ht.at[xr_, :, my_lanes])
            self.send(5, ht.at[xr_, d_high, my_lanes], left)
            self.send(6, ht.at[xr_, :, my_lanes], twin)

        def pass_far(self):
            self.arrived(3, ht.at[xf_, d_low, my_lanes])
            self.send(7, ht.at[xf_, d_low, my_lanes], twin)
            self.arrived(5, ht.at[xf_, d_high, my_lanes])
            self.send(8, ht.at[xf_, d_high, my_lanes], twin)

        def finish(self):
            for c in self.sends:
                c.wait_send()

    cos_t, sin_t = cos_ref, sin_ref
    half = D.hd // 2

    def rope(p):
        lo, hi = p[:half], p[half:]
        return jnp.concatenate([lo * cos_t[...] - hi * sin_t[...], hi * cos_t[...] + lo * sin_t[...]], axis=0)

    def project_q(l, slot, s):
        p = dot(wbuf[slot, : D.q + D.kvp, :], ht[s]).astype(BF16).astype(F32)
        for h in range(D.heads):
            qt[s, h * D.hd : (h + 1) * D.hd, :] = (rope(p[h * D.hd : (h + 1) * D.hd]) * D.hd**-0.5).astype(BF16)
        kvland[col, s] = p[D.q :].astype(BF16)

    def kv_copies():
        return [remote(kvland.at[col], kvland.at[col], kvs.at[j], kvr.at[j], row, lax.rem(col + j, n_col)) for j in range(1, n_col)]

    def kv_arrive(copies):
        for j in range(1, n_col):
            s = lax.rem(col + n_col - j, n_col)
            remote(kvland.at[s], kvland.at[s], kvs.at[j], kvr.at[j], row, col).wait_recv()
        for c in copies:
            c.wait_send()

    def key_value(l):
        def body(s, carry):
            raw = kvland[:, s].reshape(n_col * D.kvp, D.seq)
            both = dot(perm_ref[...], raw)
            zeros = jnp.zeros((128 - D.hd, D.seq), F32)
            k_nat = jnp.concatenate([rope(both[: D.hd]), zeros], axis=0).T.astype(BF16)
            v_nat = jnp.concatenate([both[D.hd :], zeros], axis=0).T.astype(BF16)
            kn[s] = k_nat
            vt[s] = both[D.hd :].astype(BF16)
            kvbuf[l, 0, s] = k_nat
            kvbuf[l, 1, s] = v_nat
            return carry

        lax.fori_loop(0, D.seqs, body, 0)

    qb = D.seq // 2

    def attention():
        def body(i, carry):
            s, h = i // D.heads, lax.rem(i, D.heads)
            q_rows = pl.ds(pl.multiple_of(h * D.hd, 16), D.hd)
            for b in range(2):
                ext = (b + 1) * qb
                lanes = slice(b * qb, (b + 1) * qb)
                sc = dot(kn[s, :ext, : D.hd], qt[s, q_rows, lanes])
                keys = lax.broadcasted_iota(jnp.int32, (ext, qb), 0)
                queries = lax.broadcasted_iota(jnp.int32, (ext, qb), 1) + b * qb
                sc = jnp.where(keys <= queries, sc, -1e30)
                p = jnp.exp(sc - jnp.max(sc, axis=0, keepdims=True))
                p = (p * (1.0 / jnp.sum(p, axis=0, keepdims=True))).astype(BF16)
                jt[s, q_rows, lanes] = dot(vt[s, :, :ext], p).astype(BF16)
            return carry

        lax.fori_loop(0, D.seqs * D.heads, body, 0)

    def gate_up(slot, j):
        def body(s, carry):
            p = dot(wbuf[slot, : 2 * fch, :], ht[s])
            g = p[:fch].astype(BF16).astype(F32)
            u = p[fch:].astype(BF16).astype(F32)
            jt[s, pl.ds(D.q + j * fch, fch), :] = (g * jax.nn.sigmoid(g) * u).astype(BF16)
            return carry

        lax.fori_loop(0, D.seqs, body, 0)

    order = (xf_, xr_, xl_, x)
    m = D.och * n_row
    m_low, m_high = pl.ds(0, m // 2), pl.ds(m // 2, m // 2)

    def add_into(dst, start, count, *srcs):
        step = 64

        def body(i, carry):
            at = pl.ds(pl.multiple_of(start + i * step, step), step)
            total = srcs[0](at).astype(F32)
            for f in srcs[1:]:
                total += f(at).astype(F32)
            dst[at, :] = total.astype(BF16)
            return carry

        lax.fori_loop(0, count // step, body, 0)

    class Reduce:
        def __init__(self, l):
            self.l = l
            self.sends = {j: [] for j in range(D.n_o)}

        def send(self, j, i, src, dst, c):
            copy = remote(src, dst, rss.at[j, i], rsr.at[j, i], row, c)
            copy.start()
            self.sends[j].append(copy)

        def arrived(self, j, i, ref):
            remote(ref, ref, rss.at[j, i], rsr.at[j, i], row, col).wait_recv()

        def stage_a(self, j, slot):
            if j >= 2:
                for c in self.sends[j - 2][:4]:
                    c.wait_send()
                self.sends[j - 2] = self.sends[j - 2][4:]
            for i, s in enumerate(order):
                ot[j % 2, s] = dot(wobuf[slot], jt[s]).astype(BF16)
                self.send(j, i, ot.at[j % 2, s, :, twin_lanes], twin_in.at[j, i], twin)

        def stage_b(self, j):
            for i, s in enumerate(order):
                self.arrived(j, i, twin_in.at[j, i])
                add_into(twin_in.at[j, i], 0, m, lambda at: ot[j % 2, s, at, my_lanes], lambda at: twin_in[j, i, at, :])
                if i == 0:
                    self.send(j, 4, twin_in.at[j, 0, m_low], far_in.at[j, m_low], right)
                    self.send(j, 5, twin_in.at[j, 0, m_high], far_in.at[j, m_high], left)

        def stage_c(self, j):
            self.arrived(j, 4, far_in.at[j, m_low])
            add_into(twin_in.at[j, 1], 0, m // 2, lambda at: twin_in[j, 1, at, :], lambda at: far_in[j, at, :])
            self.send(j, 6, twin_in.at[j, 1], near_in.at[j, 0], right)
            self.arrived(j, 5, far_in.at[j, m_high])
            add_into(twin_in.at[j, 2], m // 2, m // 2, lambda at: twin_in[j, 2, at, :], lambda at: far_in[j, at, :])
            self.send(j, 7, twin_in.at[j, 2], near_in.at[j, 1], left)

        def stage_d(self, j):
            self.arrived(j, 6, near_in.at[j, 0])
            self.arrived(j, 7, near_in.at[j, 1])
            for r in range(n_row):
                step = min(64, och)
                for a in range(0, och, step):
                    src = slice(r * och + a, r * och + a + step)
                    dst = slice(r * dr + j * och + a, r * dr + j * och + a + step)
                    u = twin_in[j, 3, src, :].astype(F32) + near_in[j, 0, src, :].astype(F32) + near_in[j, 1, src, :].astype(F32)
                    hid[dst, :] = (hid[dst, :].astype(F32) + u.astype(BF16).astype(F32)).astype(BF16)

        def finish(self):
            for j in range(D.n_o):
                for c in self.sends[j]:
                    c.wait_send()

    for l in range(D.layers):
        t0 = l * D.steps
        layer_norm(l)
        gather = Gather()
        if l > 0:
            advance()
        gather.pass_on()
        if l > 0:
            advance()
        slot = use(t0)
        gather.arrived(2, ht.at[x, :, twin_lanes])
        project_q(l, slot, x)
        gather.arrived(4, ht.at[xl_, :, twin_lanes])
        project_q(l, slot, xl_)
        gather.arrived(6, ht.at[xr_, :, twin_lanes])
        project_q(l, slot, xr_)
        gather.pass_far()
        gather.arrived(7, ht.at[xf_, d_low, twin_lanes])
        gather.arrived(8, ht.at[xf_, d_high, twin_lanes])
        project_q(l, slot, xf_)
        copies = kv_copies()
        for c in copies:
            c.start()
        gather.finish()
        gate_up(use(t0 + 1), 0)
        kv_arrive(copies)
        key_value(l)
        attention()
        for j in range(1, D.n_f):
            gate_up(use(t0 + 1 + j), j)
        red = Reduce(l)
        for j in range(D.n_o):
            slot = use(t0 + 1 + D.n_f + j)
            red.stage_a(j, slot)
            if j >= 1:
                red.stage_c(j - 1)
            if j >= 2:
                red.stage_d(j - 2)
            red.stage_b(j)
        if l + 1 < D.layers:
            advance()
        red.stage_c(D.n_o - 1)
        red.stage_d(D.n_o - 2)
        red.stage_d(D.n_o - 1)
        red.finish()

    def y_back(i):
        d = lax.rem(me + i, n)
        return remote(hid.at[pl.ds(pl.multiple_of(d * dl, 16), dl), :], piece_of(y_out, me), xs.at[i], xr.at[i], d // n_col, lax.rem(d, n_col))

    own_y = pltpu.make_async_copy(hid.at[pl.ds(pl.multiple_of(me * dl, 16), dl), :], piece_of(y_out, me), xr.at[0])
    own_y.start()

    def y_start(i, carry):
        y_back(i).start()
        return carry

    lax.fori_loop(1, n, y_start, 0)

    def kv_back(i):
        r = lax.rem(row + i, n_row)
        pos = pl.ds(pl.multiple_of((r * n_col + col) * D.pos, 16), D.pos)
        return kvbuf.at[:, :, :, pos, :], kv_out.at[:, :, pl.ds(row * D.seqs, D.seqs)], r

    src, dst, _ = kv_back(0)
    own_kv = pltpu.make_async_copy(src, dst, fl)
    own_kv.start()
    kv_sends = []
    for i in range(1, n_row):
        src, dst, r = kv_back(i)
        c = remote(src, dst, fs.at[i], fr.at[i], r, col)
        c.start()
        kv_sends.append(c)

    def y_finish(i, carry):
        s = lax.rem(me + n - i, n)
        remote(piece_of(y_out, s), piece_of(y_out, s), xs.at[i], xr.at[i], row, col).wait_recv()
        y_back(i).wait_send()
        return carry

    lax.fori_loop(1, n, y_finish, 0)
    own_y.wait()
    own_kv.wait()
    for i in range(1, n_row):
        r = lax.rem(row + n_row - i, n_row)
        dst = kv_out.at[:, :, pl.ds(r * D.seqs, D.seqs)]
        remote(dst, dst, fs.at[i], fr.at[i], row, col).wait_recv()
    for c in kv_sends:
        c.wait_send()
    for t in sorted(pending):
        drain(t)


def solution(mesh):
    n_row, n_col = mesh.shape["row"], mesh.shape["col"]
    group = n_row * n_col
    act_spec = P("dp", None, ("row", "col"))
    weight_spec = P(None, "row", "col")

    def device_fn(x_loc, gain_loc, w_in_loc, w_kv_loc, w_out_loc):
        D = Dims()
        D.n_row, D.n_col = n_row, n_col
        n_batch, D.seq, D.dl = x_loc.shape
        D.layers, D.dr, e = w_in_loc.shape
        D.d = D.dl * group
        r_block = w_out_loc.shape[1]
        D.f = e - r_block
        D.q = r_block - D.f
        kv_local = w_kv_loc.shape[2]
        D.hd = kv_local * n_col // 2
        D.heads = D.q // D.hd
        D.kvp = 32
        D.tok = n_batch * D.seq // group
        D.seqs = n_batch // n_row
        D.pos = D.seq // group
        D.fch = min(256, D.f)
        D.n_f = D.f // D.fch
        D.och = min(128, D.dr)
        D.n_o = D.dr // D.och
        D.steps = 1 + D.n_f + D.n_o
        assert D.seq == 2 * D.tok and D.seqs == n_col // 2

        half = D.hd // 2
        inv_freq = (np.float32(1.0) / (np.float32(10000.0) ** (np.arange(half, dtype=np.float32) * np.float32(2.0) / np.float32(D.hd)))).astype(np.float32)
        angles = (inv_freq[:, None] * np.arange(D.seq, dtype=np.float32)[None, :]).astype(np.float32)
        cos_t, sin_t = np.cos(angles).astype(np.float32), np.sin(angles).astype(np.float32)
        perm = np.zeros((2 * D.hd, n_col * D.kvp), np.float32)
        for i in range(2 * D.hd):
            perm[i, (i // kv_local) * D.kvp + i % kv_local] = 1.0

        x_t = x_loc.transpose(0, 2, 1)
        w_t = w_in_loc.transpose(0, 2, 1)
        wkv_t = jnp.pad(w_kv_loc.transpose(0, 2, 1), ((0, 0), (0, D.kvp - kv_local), (0, 0)))
        wo_t = w_out_loc.transpose(0, 2, 1)
        gains = jnp.pad(gain_loc, ((0, 16 - D.layers), (0, 128 - D.dl)))

        m = D.och * n_row
        sds = jax.ShapeDtypeStruct
        dma = pltpu.SemaphoreType.DMA
        out = pl.pallas_call(
            functools.partial(kernel, D),
            out_shape=(
                sds(x_t.shape, BF16),
                sds((D.layers, 2, n_batch, D.pos, 128), BF16),
                sds((D.layers, e, D.d), BF16),
                sds((D.layers, D.kvp, D.d), BF16),
                sds((D.layers, n_row, D.dr, r_block), BF16),
            ),
            in_specs=[ANY] * 5 + [VMEM] * 3,
            out_specs=(ANY,) * 5,
            scratch_shapes=[
                pltpu.VMEM((group, D.dl, D.tok), BF16),
                pltpu.VMEM((group, 16, 128), BF16),
                pltpu.VMEM((D.layers, D.d, 128), F32),
                pltpu.VMEM((D.d, D.tok), BF16),
                pltpu.VMEM((D.seqs, D.d, D.seq), BF16),
                pltpu.VMEM((2, max(2 * D.fch, D.q + D.kvp), D.d), BF16),
                pltpu.VMEM((2, m, r_block), BF16),
                pltpu.VMEM((D.seqs, D.q, D.seq), BF16),
                pltpu.VMEM((n_col, D.seqs, D.kvp, D.seq), BF16),
                pltpu.VMEM((D.seqs, D.seq, 128), BF16),
                pltpu.VMEM((D.seqs, D.hd, D.seq), BF16),
                pltpu.VMEM((D.layers, 2, D.seqs, D.seq, 128), BF16),
                pltpu.VMEM((D.seqs, r_block, D.seq), BF16),
                pltpu.VMEM((2, D.seqs, m, D.seq), BF16),
                pltpu.VMEM((D.n_o, 4, m, D.tok), BF16),
                pltpu.VMEM((D.n_o, m, D.tok), BF16),
                pltpu.VMEM((D.n_o, 2, m, D.tok), BF16),
                dma((group,)), dma((group,)), dma((group,)), dma((group,)),
                dma((SLOTS, 4, 3)), dma((SLOTS, 4, 3)),
                dma((9,)), dma((9,)),
                dma((n_col,)), dma((n_col,)),
                dma((D.n_o, 8)), dma((D.n_o, 8)),
                dma((2, 8)),
                dma((n_row,)), dma((n_row,)), dma,
            ],
            compiler_params=pltpu.CompilerParams(collective_id=0, has_side_effects=True, vmem_limit_bytes=67_000_000),
            name="two_layers",
        )(x_t, gains, w_t, wkv_t, wo_t, jnp.asarray(cos_t), jnp.asarray(sin_t), jnp.asarray(perm, BF16))
        return out[0].transpose(0, 2, 1), out[1][..., : D.hd]

    return jax.shard_map(device_fn, mesh=mesh, in_specs=(act_spec, P(None, ("row", "col")), weight_spec, weight_spec, P(None, "col", "row")), out_specs=(act_spec, P(None, None, "dp", ("row", "col"), None)), check_vma=False)
```

time: 2360 us -> 501 us (0.21)
  waiting for transfers between devices: 1790 us -> 0 us
  Pallas kernels: 0 us -> 477 us
  matrix products: 259 us -> 0 us
  blocking collectives: 183 us -> 0 us
  other arithmetic: 88.5 us -> 0 us
    psum x2 -> x0, waiting for transfers between devices: 1570 us -> none  [device_fn(): main_proj, kv_piece = lax.psum((part_main, part_kv), 'row')]
    pallas_call x0 -> x1, Pallas kernels: none -> 477 us  [device_fn(): pl.pallas_call(functools.partial(kernel, D), out_shape=(sds(x_t.shape, BF...]
    dot_general x8 -> x0, matrix products: 215 us -> none  [the longest x2 89.8 us: device_fn(): jnp.einsum('bsd,de->bse', normed_row, w_in_loc[layer_idx], preferred_elem...]
    psum x4 -> x0, blocking collectives: 183 us -> none  [the longest x2 95.7 us: device_fn(): lax.psum(jnp.sum(hidden_f32, axis=-1, keepdims=True), ('row', 'col'))]
    reduce_scatter x2 -> x0, waiting for transfers between devices: 112 us -> none  [device_fn(): update = lax.psum_scatter(part_out, 'col', scatter_dimension=2, tiled=True)]
    all_gather x4 -> x0, waiting for transfers between devices: 108 us -> none  [the longest x2 108 us: device_fn(): normed_row = lax.all_gather(normed, 'col', axis=2, tiled=True)]
    convert_element_type x10 -> x0, other arithmetic: 62.8 us -> none  [the longest x2 52.6 us: device_fn(): (jax.nn.silu(gate_val.astype(jnp.float32)) * up_val.astype(jnp.float32))....]
    sub x2 -> x0, matrix products: 44.4 us -> none  [device_fn(): attn_prob = jax.nn.softmax(scores, axis=-1).astype(jnp.bfloat16)]
  transfers between devices with their start and end apart: 8 -> 0, of which waited for: 6 -> 0; matrix products, arithmetic and copies ran while one was open for 3% -> 0% of each run, Pallas kernels for 0% -> 0%
where the time goes in v2:
time: 501 us; the launch traced here: 492 us
  Pallas kernels  477 us (95%)
  local copies, waits for them, and re-layouts  13.7 us (3%)
    pallas_call x1, Pallas kernels, device_fn(): pl.pallas_call(functools.partial(kernel, D), out_shape=(sds(x_t.shape, BF...  477 us
    unnamed x4, local copies, waits for them, and re-layouts  11.8 us

profile of v2, /device:TPU:97, one launch (start us, length us, event | category | flops | bytes accessed | tf_op | source)
XLA Modules:
  0.0 491.9 jit_solution(3065442771795710358)
XLA Ops:
  0.6 1.3 pad.8.gains
  1.9 0.8 copy.13
  2.7 0.6 pad.9.wkv_t
  3.3 6.9 %copy.11 = bf16[2,1600,640]{1,2,0:T(8,128)(2,1)} copy(bf16[2,1600,640]{2,1,0:T(8,128)(2,1)} %param.12) | data formatting | bytes 8192000 | tf_op args[4]
  10.2 477.1 %two_layers.1 = (bf16[16,80,512]{2,1,0:T(8,128)(2,1)}, bf16[2,2,16,16,128]{4,3,2,1,0:T(8,128)(2,1)}, bf16[2,2880,2560]{2,1,0:T(8,128)(2,1)}, bf16[2,32,2560]{2,1,0:T(8,128)(2,1)}, bf16[2,4,640,1600]{3,2,1,0:T(8,128)(2,1)}) custom-call(bf16[16,80,512]{2,1,0:T(8,128)(2,1)} %bitcast.10, bf16[16,128]{1,0:T(8,128)(2,1)} %pad.8.gains, ...), custom_call_target="tpu_custom_call" | custom-call | tf_op jit(solution)/shard_map/two_layers/pallas_call | solution.py:571
  487.3 2.5 copy.16
  489.8 1.7 copy.17
